TPU v7x, 512 devices: a 4x2x32 block of a 4x16x32 slice. The times are simulated.
512 devices in a mesh: groups: 2 (over y), band: 64 (over z, core), chan: 4 (over x).
Axes of the slice: x: 4, y: 2, z: 32, core: 2. Of those that a mesh axis runs over, the one named last changes fastest.
The devices are a block of a 4x16x32 slice.
Arguments:
- slide_region: float32 [16, 512, 8192], P('chan', ('groups', 'band')), parts along dimension 1, may hold values from -6 to 6
- row_taps: float32 [16, 257], P('chan'), may hold values from -0.375 to 0.375
- column_taps: float32 [16, 257], replicated, may hold values from -0.375 to 0.375
- channel_mix: float32 [16, 16], replicated, may hold values from -1.5 to 1.5
Outputs:
- filtered: float32 [16, 512, 8192], P('chan', ('groups', 'band')), parts along dimension 1
There are 2 independent parts, one for each index of `groups`. A program takes and returns all parts, laid end to end along the dimension named above; an argument that names none is the same for every part. Nothing has to cross between parts.
All inputs are finite; a program needn't handle non-finite values.
Results may differ from a plain program's by a relative error of at most 0.00007.
Values sent between devices are 32-bit elements; how exact they have to be, the bound alone decides.
A program may use at most 64 MiB of HBM per device.

v0:
```python
import jax
import jax.numpy as jnp
from jax import lax
from jax.sharding import Mesh
from jax.sharding import PartitionSpec as P

BAND = ("band_0", "band_1")
GROUPS_BAND = ("groups", "band_0", "band_1")


precise = lax.Precision.HIGHEST


def cut_along(value, dim, size):
    before, after = (value.shape[:dim], value.shape[dim + 1 :])
    return jnp.moveaxis(value.reshape(*before, size, -1, *after), dim, 0)


def joined_along(parts, dim):
    shape = list(parts.shape[1:])
    shape[dim] *= parts.shape[0]
    return jnp.moveaxis(parts, 0, dim).reshape(shape)


def moved_by_axis(parts, axes, sequence):
    shape = [lax.axis_size(a) for a in axes]
    parts = parts.reshape(*shape, *parts.shape[1:])
    for k in sequence:
        parts = lax.all_to_all(parts, axes[k], split_axis=k, concat_axis=k, tiled=True)
    return parts.reshape(-1, *parts.shape[len(axes) :])


def core_and_chips(value, groups, sequence, split_dim, concat_dim):
    size = lax.axis_size(groups[0]) * lax.axis_size(groups[1])
    parts = cut_along(value, split_dim, size)
    return joined_along(moved_by_axis(parts, groups, sequence), concat_dim)


def sent_to_all(value, axis):
    size = lax.axis_size(axis)
    return lax.all_to_all(
        jnp.broadcast_to(value[None], (size, *value.shape)), axis, 0, 0, tiled=True
    )


def gathered_copies(value, axis, dim):
    return joined_along(sent_to_all(value, axis), dim)


def band_tables(filter_taps, tile_size):
    channels, length = filter_taps.shape
    margin = (length - 1) // 2
    period = 4 * tile_size
    border = 3 * tile_size + length
    widened = jnp.pad(filter_taps, ((0, 0), (border, border)))
    lowest = margin - tile_size + border
    window = widened[:, lowest : lowest + 3 * tile_size]
    vector = jnp.pad(window, ((0, 0), (0, tile_size)))
    repeated = jnp.tile(vector, (1, tile_size))[:, : tile_size * (period - 1)]
    toeplitz = repeated.reshape(channels, tile_size, period - 1)[:, :, : 3 * tile_size]
    stacked = jnp.transpose(toeplitz, (0, 2, 1))
    return stacked.reshape(channels, 3, tile_size, tile_size)


def along_columns(signal, filter_taps):
    tile_size = 128
    tables = band_tables(filter_taps, tile_size)
    channels, row_count, col_count = signal.shape
    tile_count = col_count // tile_size
    tiled = signal.reshape(channels, row_count, tile_count, tile_size)
    padded = jnp.pad(tiled, ((0, 0), (0, 0), (1, 1), (0, 0)))
    result = jnp.einsum(
        "crti,cij->crtj", padded[:, :, 0:tile_count], tables[:, 0], precision=precise
    )
    result = result + jnp.einsum(
        "crti,cij->crtj", padded[:, :, 1 : tile_count + 1], tables[:, 1], precision=precise
    )
    result = result + jnp.einsum(
        "crti,cij->crtj", padded[:, :, 2:], tables[:, 2], precision=precise
    )
    return result.reshape(channels, row_count, col_count)


def along_rows(signal, filter_taps):
    channels, row_count, col_count = signal.shape
    tile_size = 128
    tables = band_tables(filter_taps, tile_size)
    tile_count = row_count // tile_size
    tiled = signal.reshape(channels, tile_count, tile_size, col_count)
    padded = jnp.pad(tiled, ((0, 0), (1, 1), (0, 0), (0, 0)))
    result = jnp.einsum("ctiw,cij->ctjw", padded[:, 0:tile_count], tables[:, 0], precision=precise)
    result = result + jnp.einsum(
        "ctiw,cij->ctjw", padded[:, 1 : tile_count + 1], tables[:, 1], precision=precise
    )
    result = result + jnp.einsum("ctiw,cij->ctjw", padded[:, 2:], tables[:, 2], precision=precise)
    return result.reshape(channels, row_count, col_count)


def on_device(slide_region, row_taps, column_taps, channel_mix):
    local_channels = slide_region.shape[0]
    across = along_columns(slide_region, row_taps)
    column_band = core_and_chips(across, ("band_0", "band_1"), (1, 0), 2, 1)
    first_channel = lax.axis_index("chan") * local_channels
    own_taps = lax.dynamic_slice_in_dim(column_taps, first_channel, local_channels, 0)
    vertical = along_rows(column_band, own_taps)
    own_mixing = lax.dynamic_slice_in_dim(channel_mix, first_channel, local_channels, 0)
    blended = jnp.einsum(
        "oc,chw->ohw", own_mixing, gathered_copies(vertical, "chan", 0), precision=precise
    )
    return lax.all_to_all(blended, BAND, split_axis=1, concat_axis=2, tiled=True)


def solution(mesh):
    split = Mesh(
        mesh.devices.reshape(mesh.shape["groups"], 32, 2, mesh.shape["chan"]),
        ("groups", "band_0", "band_1", "chan"),
    )
    in_specs = (P("chan", GROUPS_BAND, None), P("chan", None), P(), P())
    out_specs = P("chan", GROUPS_BAND, None)
    return jax.shard_map(
        on_device, mesh=split, in_specs=in_specs, out_specs=out_specs, check_vma=False
    )
```

profile of v0, /device:TPU:40, one launch (start us, length us, event | category | flops | bytes accessed | tf_op | source)
XLA Modules:
  0.0 228.5 jit_solution(11120295280329860627)
XLA Ops:
  0.0 0.0 copy-start
  0.0 0.7 pad_slice_fusion.8
  0.7 1.4 reshape.35
  2.1 0.1 broadcast_bitcast_fusion
  2.2 0.7 copy.60
  2.9 0.1 slice.69
  3.0 1.0 reshape.36
  4.0 0.1 slice_bitcast_fusion
  4.1 0.3 copy.34
  4.4 0.6 convolution_bitcast_fusion.1
  5.0 0.6 convolution_bitcast_fusion
  5.6 0.6 fusion.1
  6.3 0.1 copy.38
  6.3 4.2 %all_to_all.33 = f32[32,2,4,4,128]{4,0,3,2,1:T(8,128)S(1)} all-to-all(f32[32,2,4,4,128]{4,0,3,2,1:T(8,128)S(1)} %copy.38), channel_id=1, replica_groups=mesh['groups'=2,'band_0'=32,'band_1'=2,'chan'=4] {'band_1'}, dimensions={1} | all-to-all | bytes 1048576 | tf_op jit(solution)/shard_map/all_to_all | solution.py:29
  10.5 1.2 copy.39
  11.7 45.8 %all-to-all-start.1 = ((f32[32,2,4,4,128]{4,1,3,2,0:T(2,128)}), f32[32,2,4,4,128]{4,1,3,2,0:T(2,128)S(1)}, u32[]{:S(2)}, u32[]{:S(2)}) async-start(f32[32,2,4,4,128]{4,1,3,2,0:T(2,128)} %copy.39), calls=%async_computation.1 | async-start | bytes 1048576 | tf_op jit(solution)/shard_map/all_to_all | solution.py:29
  57.5 0.0 copy-done
  57.5 0.1 broadcast_bitcast_fusion.1
  57.6 0.7 copy.59
  58.3 0.1 slice.66
  58.4 1.0 reshape.33
  59.4 0.1 slice_bitcast_fusion.1
  59.5 0.3 copy.32
  59.8 62.3 %all-to-all-done.1 = f32[32,2,4,4,128]{4,1,3,2,0:T(2,128)S(1)} async-done(((f32[32,2,4,4,128]{4,1,3,2,0:T(2,128)}), f32[32,2,4,4,128]{4,1,3,2,0:T(2,128)S(1)}, u32[]{:S(2)}, u32[]{:S(2)}) %all-to-all-start.1) | async-done | bytes 524320 | tf_op jit(solution)/shard_map/all_to_all | solution.py:29
  122.1 0.3 copy.40
  122.4 0.3 copy.41
  122.7 0.6 fusion.2
  123.3 0.6 convolution_add_fusion.1
  124.0 0.6 convolution_add_fusion
  124.6 0.3 copy.44
  125.0 0.3 broadcast_in_dim.8
  125.2 30.0 %all_to_all.34 = f32[4,4,256,128]{3,1,2,0:T(4,128)S(1)} all-to-all(f32[4,4,256,128]{3,1,2,0:T(4,128)S(1)} %broadcast_in_dim.8), channel_id=1, replica_groups=mesh['groups'=2,'band_0'=32,'band_1'=2,'chan'=4] {'chan'}, dimensions={0} | all-to-all | bytes 4194304 | tf_op jit(solution)/shard_map/all_to_all | solution.py:41
  155.2 0.4 copy.45
  155.6 1.8 fusion.3
  157.4 69.9 %all_to_all.35 = f32[4,256,128]{2,0,1:T(4,128)S(1)} all-to-all(f32[4,256,128]{2,0,1:T(4,128)S(1)} %fusion.3), channel_id=1, replica_groups=mesh['groups'=2,'band_0'=32,'band_1'=2,'chan'=4] {'band_0','band_1'}, dimensions={1} | all-to-all | bytes 1048576 | tf_op jit(solution)/shard_map/all_to_all | solution.py:110
  227.3 0.2 copy.46
  227.5 1.0 all_to_all.28
  (4 shorter events, 0.0 us)
Async XLA Ops:
  0.0 57.5 %copy-start = (f32[16,257]{1,0:T(8,128)S(1)}, f32[16,257]{1,0:T(8,128)}, u32[]{:S(2)}) copy-start(f32[16,257]{1,0:T(8,128)} %param.6) | copy-start | bytes 49348
  11.7 110.4 %all-to-all-start.1 = ((f32[32,2,4,4,128]{4,1,3,2,0:T(2,128)}), f32[32,2,4,4,128]{4,1,3,2,0:T(2,128)S(1)}, u32[]{:S(2)}, u32[]{:S(2)}) async-start(f32[32,2,4,4,128]{4,1,3,2,0:T(2,128)} %copy.39), calls=%async_computation.1 | async-start | bytes 1048576 | tf_op jit(solution)/shard_map/all_to_all | solution.py:29
where the time goes:
time: 229 us; the launch traced here: 228 us
  blocking collectives  104 us (45%)
  waiting for transfers between devices  62.3 us (27%)
  starting transfers between devices  45.8 us (20%)
  local copies, waits for them, and re-layouts  10.5 us (5%)
  matrix products  5.56 us (2%)
    all_to_all x1, blocking collectives, on_device(): lax.all_to_all(blended, BAND, split_axis=1, concat_axis=2, tiled=True)  69.9 us
    all_to_all x1, waiting for transfers between devices, moved_by_axis(): lax.all_to_all(parts, axes[k], split_axis=k, concat_axis=k, tiled=True)  62.3 us
    all_to_all x1, starting transfers between devices, moved_by_axis(): lax.all_to_all(parts, axes[k], split_axis=k, concat_axis=k, tiled=True)  45.8 us
    all_to_all x1, blocking collectives, sent_to_all(): lax.all_to_all(jnp.broadcast_to(value[None], (size, *value.shape)), axis,...  30 us
  transfers between devices with their start and end apart: 1, of which 1 were waited for; matrix products, arithmetic and copies ran while one was open for 1% of the time, Pallas kernels for 0%

commit v1 on v0

v1 whole, which is shorter than its diff:
```python
import functools

import jax
import jax.numpy as jnp
from jax import lax
from jax.experimental import pallas as pl
from jax.experimental.pallas import tpu as pltpu
from jax.sharding import PartitionSpec as P

MESH = pl.DeviceIdType.MESH
F32 = jnp.float32
BF16 = jnp.bfloat16
LANES = 128
HALF = 64


def two_parts(value):
    high = value.astype(BF16)
    low = (value - high.astype(F32)).astype(BF16)
    return high, low


def three_products(dot, left, right):
    (lh, ll), (rh, rl) = left, right
    return dot(lh, rh) + (dot(lh, rl) + dot(ll, rh))


def dot_nt(a, b):
    return lax.dot_general(a, b, (((1,), (1,)), ((), ())), preferred_element_type=F32)


def dot_nn(a, b):
    return lax.dot_general(a, b, (((1,), (0,)), ((), ())), preferred_element_type=F32)


def banded(row, count, width, shift):
    return pltpu.roll(jnp.broadcast_to(row, (count, width)), shift % width, 1, stride=1, stride_axis=0)


def kernel(
    bands, chans, x_ref, row_ref, col_ref, mix_ref, out_ref,
    taps, padded, row_high, row_low, sent, landed, col_high, col_low, coefs,
    gathered, mixed, returned,
    send_sems, recv_sems,
):
    me = lax.axis_index("band")
    my_z, my_core = me // 2, lax.rem(me, 2)
    my_x = lax.axis_index("chan")
    zs = bands // 2
    tiles = x_ref.shape[2] // LANES
    rows = x_ref.shape[1]
    height = bands * rows

    def band_peer(i):
        q, other = i // 2, lax.rem(i, 2)
        distance = zs // 2 - (q + 1) // 2
        z = lax.rem(my_z + distance * (2 * lax.rem(q, 2) - 1) + zs, zs)
        return z * 2 + lax.rem(my_core + other, 2)

    def chan_peer(j):
        return lax.rem(my_x + 1 + j, chans)

    barrier = pltpu.get_barrier_semaphore()

    def greet(i, _):
        pl.semaphore_signal(barrier, inc=1, device_id={"band": peer_of(i)}, device_id_type=MESH)
        return 0

    def peer_of(i):
        last = i // (bands - 2)
        return last * (me + 1 - 2 * my_core) + (1 - last) * band_peer(i)

    lax.fori_loop(0, bands - 1, greet, 0)
    for j in range(chans - 1):
        pl.semaphore_signal(barrier, inc=1, device_id={"chan": chan_peer(j)}, device_id_type=MESH)

    lane = lax.broadcasted_iota(jnp.int32, (1, 1, LANES), 2)
    left = lane < HALF
    sub = lax.broadcasted_iota(jnp.int32, (1, 2 * rows, 1), 1)
    upper = sub < rows

    taps[...] = jnp.zeros_like(taps)
    taps[0:4, 0:257] = row_ref[...]
    for c in range(4):
        table = banded(taps[c : c + 1, 0 : 3 * LANES], LANES, 3 * LANES, 0)
        high, low = two_parts(table)
        where = pl.ds((c % 2) * LANES, LANES)
        row_high[c // 2, where] = high
        row_low[c // 2, where] = low
    zero = jnp.zeros((2 * rows, LANES), F32)
    for p in range(2):
        padded[p, 0] = zero
        padded[p, tiles + 1] = zero
        for t in range(tiles):
            for c in range(2):
                padded[p, t + 1, c * rows : (c + 1) * rows] = x_ref[2 * p + c, :, t * LANES : (t + 1) * LANES]

    block = 16

    def filter_rows(n, _):
        t = n * block
        out = []
        for p in range(2):
            near = [padded[p, pl.ds(t + s, block)].reshape(block * 2 * rows, LANES) for s in range(3)]
            both = three_products(
                dot_nt, two_parts(jnp.concatenate(near, axis=1)), (row_high[p], row_low[p])
            )
            both = both.reshape(block, 2 * rows, 2 * LANES)
            out.append(jnp.where(upper, both[:, :, :LANES], both[:, :, LANES:]))
        sent[0, pl.ds(t, block)] = jnp.where(left, out[0], pltpu.roll(out[1], HALF, 2))
        sent[1, pl.ds(t, block)] = jnp.where(left, pltpu.roll(out[0], HALF, 2), out[1])
        return 0

    lax.fori_loop(0, tiles // block, filter_rows, 0)

    pl.semaphore_wait(barrier, bands - 1 + chans - 1)

    def out_to_bands(source, target, phase, k):
        def send(i, _):
            b = peer_of(i)
            pltpu.make_async_remote_copy(
                source.at[k, b], target.at[k, me], send_sems.at[phase, k], recv_sems.at[phase, k],
                device_id={"band": b}, device_id_type=MESH,
            ).start()
            return 0

        lax.fori_loop(0, bands - 1, send, 0)

    def all_bands(ref, sems, phase, k):
        view = ref.at[k, pl.ds(0, bands - 1)]
        pltpu.make_async_copy(view, view, sems.at[phase, k]).wait()

    def all_chans(sems, k):
        view = gathered.at[k, pl.ds(0, chans - 1)]
        pltpu.make_async_copy(view, view, sems.at[1, k]).wait()

    for k in range(2):
        out_to_bands(sent, landed, 0, k)
        landed[k, me] = sent[k, me]

    for c in range(4):
        taps[4:5, 0:257] = col_ref[pl.ds(my_x * 4 + c, 1), :]
        table = banded(taps[4:5, 0 : 2 * height], height, 2 * height, -(height // 2))[:, :height]
        high, low = two_parts(table)
        where = pl.ds((c // 2) * height, height)
        col_high[c % 2, where] = high
        col_low[c % 2, where] = low
    wide = lax.broadcasted_iota(jnp.int32, (8, LANES), 1) < HALF
    for o in range(2):
        for g in range(4 * chans // 2):
            first, second = 4 * (g // 2) + g % 2, 4 * (g // 2) + g % 2 + 2
            lo, hi = my_x * 4 + o, my_x * 4 + 2 + o
            coefs[o, g, 0] = jnp.where(wide, mix_ref[lo, first], mix_ref[hi, second])
            coefs[o, g, 1] = jnp.where(wide, mix_ref[lo, second], mix_ref[hi, first])

    for k in range(2):
        all_bands(landed, recv_sems, 0, k)
        tall = landed[k].reshape(bands // 2, 2, 2 * rows, LANES)
        even, odd = tall[:, 0], tall[:, 1]
        picked = (
            jnp.where(upper, even, pltpu.roll(odd, rows, 1)),
            jnp.where(upper, pltpu.roll(even, rows, 1), odd),
        )
        for c in range(2):
            signal = two_parts(picked[c].reshape(height, LANES))
            both = three_products(dot_nn, (col_high[c], col_low[c]), signal)
            gathered[k, my_x, c] = jnp.where(left[0], both[:height], both[height:])
        for j in range(chans - 1):
            pltpu.make_async_remote_copy(
                gathered.at[k, my_x], gathered.at[k, my_x], send_sems.at[1, k], recv_sems.at[1, k],
                device_id={"chan": chan_peer(j)}, device_id_type=MESH,
            ).start()
        all_chans(recv_sems, k)

        def mix_rows(n, _):
            total = [None, None]
            for g in range(2 * chans):
                value = gathered[k, g // 2, g % 2, pl.ds(pl.multiple_of(n * 8, 8), 8)]
                swapped = pltpu.roll(value, HALF, 1)
                for o in range(2):
                    term = coefs[o, g, 0] * value + coefs[o, g, 1] * swapped
                    total[o] = term if total[o] is None else total[o] + term
            first = upper[0]
            mixed[k, 2 * n] = jnp.where(first, total[0], pltpu.roll(total[1], rows, 0))
            mixed[k, 2 * n + 1] = jnp.where(first, pltpu.roll(total[0], rows, 0), total[1])
            return 0

        lax.fori_loop(0, height // 8, mix_rows, 0)
        out_to_bands(mixed, returned, 2, k)
        returned[k, me] = mixed[k, me]

    for k in range(2):
        all_bands(returned, recv_sems, 2, k)
    for t in range(tiles):
        a, b = returned[0, t], returned[1, t]
        keep = left[0]
        pair = (
            jnp.where(keep, a, pltpu.roll(b, HALF, 1)),
            jnp.where(keep, pltpu.roll(a, HALF, 1), b),
        )
        for p in range(2):
            for o in range(2):
                out_ref[2 * p + o, :, t * LANES : (t + 1) * LANES] = pair[p][o * rows : (o + 1) * rows]

    for k in range(2):
        all_bands(landed, send_sems, 0, k)
        all_chans(send_sems, k)
        all_bands(returned, send_sems, 2, k)


def on_device(bands, chans, slide_region, row_taps, column_taps, channel_mix):
    channels, rows, cols = slide_region.shape
    tiles = cols // LANES
    height = bands * rows
    vmem = pl.BlockSpec(memory_space=pltpu.VMEM)
    moved = pltpu.VMEM((2, bands, 2 * rows, LANES), F32)
    return pl.pallas_call(
        functools.partial(kernel, bands, chans),
        out_shape=jax.ShapeDtypeStruct(slide_region.shape, F32),
        in_specs=[vmem, vmem, vmem, pl.BlockSpec(memory_space=pltpu.SMEM)],
        out_specs=vmem,
        scratch_shapes=[
            pltpu.VMEM((8, 2 * height), F32),
            pltpu.VMEM((2, tiles + 2, 2 * rows, LANES), F32),
            pltpu.VMEM((2, 2 * LANES, 3 * LANES), BF16),
            pltpu.VMEM((2, 2 * LANES, 3 * LANES), BF16),
            moved,
            moved,
            pltpu.VMEM((2, 2 * height, height), BF16),
            pltpu.VMEM((2, 2 * height, height), BF16),
            pltpu.VMEM((2, 2 * chans, 2, 8, LANES), F32),
            pltpu.VMEM((2, chans, 2, height, LANES), F32),
            moved,
            moved,
            pltpu.SemaphoreType.DMA((3, 2)),
            pltpu.SemaphoreType.DMA((3, 2)),
        ],
        compiler_params=pltpu.CompilerParams(collective_id=0, has_side_effects=True),
    )(slide_region, row_taps, column_taps, channel_mix)


def solution(mesh):
    in_specs = (P("chan", ("groups", "band"), None), P("chan", None), P(), P())
    out_specs = P("chan", ("groups", "band"), None)
    return jax.shard_map(
        functools.partial(on_device, mesh.shape["band"], mesh.shape["chan"]),
        mesh=mesh, in_specs=in_specs, out_specs=out_specs, check_vma=False,
    )
```

time: 229 us -> 150 us (0.66)
  Pallas kernels: 0 us -> 147 us
  blocking collectives: 104 us -> 0 us
  waiting for transfers between devices: 62.3 us -> 0 us
  starting transfers between devices: 45.8 us -> 0 us
  local copies, waits for them, and re-layouts: 10.5 us -> 1.87 us
  matrix products: 5.56 us -> 0 us
    pallas_call x0 -> x1, Pallas kernels: none -> 147 us  [on_device(): pl.pallas_call(functools.partial(kernel, bands, chans), out_shape=jax.Sha...]
    all_to_all x3 -> x0, blocking collectives: 104 us -> none  [the longest x1 69.9 us: on_device(): lax.all_to_all(blended, BAND, split_axis=1, concat_axis=2, tiled=True)]
    all_to_all x1 -> x0, waiting for transfers between devices: 62.3 us -> none  [moved_by_axis(): lax.all_to_all(parts, axes[k], split_axis=k, concat_axis=k, tiled=True)]
    all_to_all x1 -> x0, starting transfers between devices: 45.8 us -> none  [moved_by_axis(): lax.all_to_all(parts, axes[k], split_axis=k, concat_axis=k, tiled=True)]
    dot_general x7 -> x0, matrix products: 5.56 us -> none  [the longest x1 1.8 us: on_device(): jnp.einsum('oc,chw->ohw', own_mixing, gathered_copies(vertical, 'chan', 0...]
    reshape x4 -> x0, local copies, waits for them, and re-layouts: 3.46 us -> none  [the longest x2 2 us: band_tables(): repeated.reshape(channels, tile_size, period - 1)[:, :, :3 * tile_size]]
    all_to_all x5 -> x0, local copies, waits for them, and re-layouts: 3 us -> none  [the longest x2 1.46 us: moved_by_axis(): lax.all_to_all(parts, axes[k], split_axis=k, concat_axis=k, tiled=True)]
  transfers between devices with their start and end apart: 1 -> 0, of which waited for: 1 -> 0; matrix products, arithmetic and copies ran while one was open for 1% -> 0% of each run, Pallas kernels for 0% -> 0%
where the time goes in v1:
time: 150 us; the launch traced here: 149 us
  Pallas kernels  147 us (98%)
  local copies, waits for them, and re-layouts  1.87 us (1%)
    pallas_call x1, Pallas kernels, on_device(): pl.pallas_call(functools.partial(kernel, bands, chans), out_shape=jax.Sha...  147 us

profile of v1, /device:TPU:40, one launch (start us, length us, event | category | flops | bytes accessed | tf_op | source)
XLA Modules:
  0.0 149.2 jit_solution(7713292748222896325)
XLA Ops:
  0.0 147.4 %shard_map.46 = f32[4,4,8192]{2,1,0:T(4,128)} custom-call(f32[4,4,8192]{2,1,0:T(4,128)} %x_ref.1, f32[4,257]{1,0:T(4,128)} %row_ref.1, f32[16,257]{1,0:T(8,128)} %col_ref.1, f32[16,16]{1,0:T(8,128)} %mix_ref.1), custom_call_target="tpu_custom_call" | custom-call | tf_op jit(solution)/shard_map/pallas_call | solution.py:217
  147.4 1.9 %copy.6 = f32[4,4,8192]{2,1,0:T(4,128)} copy(f32[4,4,8192]{2,1,0:T(4,128)} %shard_map.46) | data formatting | bytes 1048576

commit v2 on v1

v2 whole, which is shorter than its diff:
```python
import functools

import jax
import jax.numpy as jnp
from jax import lax
from jax.experimental import pallas as pl
from jax.experimental.pallas import tpu as pltpu
from jax.sharding import PartitionSpec as P

MESH = pl.DeviceIdType.MESH
F32 = jnp.float32
BF16 = jnp.bfloat16
LANES = 128
HALF = 64


def two_parts(value):
    high = value.astype(BF16)
    low = (value - high.astype(F32)).astype(BF16)
    return high, low


def three_products(dot, left, right):
    (lh, ll), (rh, rl) = left, right
    return dot(lh, rh) + (dot(lh, rl) + dot(ll, rh))


def dot_nt(a, b):
    return lax.dot_general(a, b, (((1,), (1,)), ((), ())), preferred_element_type=F32)


def dot_nn(a, b):
    return lax.dot_general(a, b, (((1,), (0,)), ((), ())), preferred_element_type=F32)


def banded(row, count, width, shift):
    return pltpu.roll(jnp.broadcast_to(row, (count, width)), shift % width, 1, stride=1, stride_axis=0)


def kernel(
    bands, chans, x_hbm, row_hbm, col_hbm, mix_hbm, out_ref,
    x_ref, row_ref, col_ref, mix_ref, taps, padded, row_high, row_low, sent, landed, col_high, col_low, coefs,
    vertical, gathered, mixed, ordered, returned,
    send_sems, recv_sems, own_sems,
):
    fetches = [
        pltpu.make_async_copy(source, target, own_sems.at[n])
        for n, (source, target) in enumerate(
            ((row_hbm, row_ref), (x_hbm, x_ref), (col_hbm, col_ref), (mix_hbm, mix_ref))
        )
    ]
    for fetch in fetches:
        fetch.start()
    me = lax.axis_index("band")
    my_z, my_core = me // 2, lax.rem(me, 2)
    my_x = lax.axis_index("chan")
    zs = bands // 2
    tiles = x_ref.shape[2] // LANES
    rows = x_ref.shape[1]
    height = bands * rows

    half = zs // 2
    partner = me + 1 - 2 * my_core

    def around(distance):
        z = lax.rem(my_z + distance + zs, zs)
        return z * 2, z * 2 + 1

    def for_all_bands(act):
        for b in around(half):
            act(b)

        def step(n, _):
            for b in (*around(half - 1 - n), *around(n + 1 - half)):
                act(b)
            return 0

        lax.fori_loop(0, half - 1, step, 0)
        act(partner)

    group = zs // 2

    def for_groups(act):
        def step(n, _):
            first = n * group + lax.rem(my_z, group)

            @pl.when(first != my_z)
            def _():
                act(first * 2)
                act(first * 2 + 1)

            @pl.when(first == my_z)
            def _():
                act(partner)

            for away in range(1, group):
                z = n * group + lax.rem(my_z + away, group)
                act(z * 2)
                act(z * 2 + 1)
            return 0

        lax.fori_loop(0, zs // group, step, 0)

    def chan_peer(j):
        return lax.rem(my_x + 1 + j, chans)

    barrier = pltpu.get_barrier_semaphore()

    def greet_any(b):
        pl.semaphore_signal(barrier, inc=1, device_id={"band": b}, device_id_type=MESH)

    for_all_bands(greet_any)
    for j in range(chans - 1):
        pl.semaphore_signal(barrier, inc=1, device_id={"chan": chan_peer(j)}, device_id_type=MESH)

    lane = lax.broadcasted_iota(jnp.int32, (1, 1, LANES), 2)
    left = lane < HALF
    sub = lax.broadcasted_iota(jnp.int32, (1, 2 * rows, 1), 1)
    upper = sub < rows

    taps[...] = jnp.zeros_like(taps)
    fetches[0].wait()
    taps[0:4, 0:257] = row_ref[...]
    for c in range(4):
        table = banded(taps[c : c + 1, 0 : 3 * LANES], LANES, 3 * LANES, 0)
        high, low = two_parts(table)
        where = pl.ds((c % 2) * LANES, LANES)
        row_high[c // 2, where] = high
        row_low[c // 2, where] = low
    fetches[1].wait()
    zero = jnp.zeros((2 * rows, LANES), F32)
    for p in range(2):
        padded[p, 0] = zero
        padded[p, tiles + 1] = zero
        for t in range(tiles):
            for c in range(2):
                padded[p, t + 1, c * rows : (c + 1) * rows] = x_ref[2 * p + c, :, t * LANES : (t + 1) * LANES]

    block = 32

    def filter_rows(n, _):
        t = n * block
        out = []
        for p in range(2):
            near = [padded[p, pl.ds(t + s, block)].reshape(block * 2 * rows, LANES) for s in range(3)]
            both = three_products(
                dot_nt, two_parts(jnp.concatenate(near, axis=1)), (row_high[p], row_low[p])
            )
            both = both.reshape(block, 2 * rows, 2 * LANES)
            out.append(jnp.where(upper, both[:, :, :LANES], both[:, :, LANES:]))
        sent[0, pl.ds(t, block)] = jnp.where(left, out[0], pltpu.roll(out[1], HALF, 2))
        sent[1, pl.ds(t, block)] = jnp.where(left, pltpu.roll(out[0], HALF, 2), out[1])
        return 0

    lax.fori_loop(0, tiles // block, filter_rows, 0)

    pl.semaphore_wait(barrier, bands - 1 + chans - 1)

    def send(source, target, phase, k, b, at=None):
        pltpu.make_async_remote_copy(
            source.at[k, b if at is None else at], target.at[k, me], send_sems.at[phase, k], recv_sems.at[phase, k],
            device_id={"band": b}, device_id_type=MESH,
        ).start()

    for_all_bands(functools.partial(send, sent, landed, 0, 0))
    for_all_bands(functools.partial(send, sent, landed, 0, 1))
    for k in range(2):
        landed[k, me] = sent[k, me]

    fetches[2].wait()
    fetches[3].wait()
    for c in range(4):
        taps[4:5, 0:257] = col_ref[pl.ds(my_x * 4 + c, 1), :]
        table = banded(taps[4:5, 0 : 2 * height], height, 2 * height, -(height // 2))[:, :height]
        high, low = two_parts(table)
        where = pl.ds((c // 2) * height, height)
        col_high[c % 2, where] = high
        col_low[c % 2, where] = low
    wide = lax.broadcasted_iota(jnp.int32, (8, LANES), 1) < HALF
    for o in range(2 * chans):
        for g in range(2 * chans):
            first, second = 4 * (g // 2) + g % 2, 4 * (g // 2) + g % 2 + 2
            lo, hi = 4 * (o // 2) + o % 2, 4 * (o // 2) + o % 2 + 2
            coefs[o, g, 0] = jnp.where(wide, mix_ref[lo, first], mix_ref[hi, second])
            coefs[o, g, 1] = jnp.where(wide, mix_ref[lo, second], mix_ref[hi, first])

    runs = zs // chans
    def wait_bytes(ref, blocks, sem):
        view = ref.at[pl.ds(0, blocks)]
        pltpu.make_async_copy(view, view, sem).wait()

    def trade(source, target, phase, k):
        for j in range(chans - 1):
            x = chan_peer(j)
            pltpu.make_async_remote_copy(
                source.at[k, x], target.at[k, my_x], send_sems.at[phase, k], recv_sems.at[phase, k],
                device_id={"chan": x}, device_id_type=MESH,
            ).start()
        target[k, my_x] = source[k, my_x]
        wait_bytes(target.at[k], chans - 1, recv_sems.at[phase, k])

    for k in range(2):
        wait_bytes(landed.at[k], bands - 1, recv_sems.at[0, k])
        tall = landed[k].reshape(bands // 2, 2, 2 * rows, LANES)
        even, odd = tall[:, 0], tall[:, 1]
        picked = (
            jnp.where(upper, even, pltpu.roll(odd, rows, 1)),
            jnp.where(upper, pltpu.roll(even, rows, 1), odd),
        )
        for c in range(2):
            signal = two_parts(picked[c].reshape(height, LANES))
            both = three_products(dot_nn, (col_high[c], col_low[c]), signal)
            filtered = jnp.where(left[0], both[:height], both[height:])
            filtered = filtered.reshape(runs, chans, 2 * rows, LANES)
            for x in range(chans):
                vertical[k, x, c] = filtered[:, x]
        trade(vertical, gathered, 1, k)

        def mix_run(n, _):
            values = [gathered[k, g // 2, g % 2, n] for g in range(2 * chans)]
            swapped = [pltpu.roll(value, HALF, 1) for value in values]
            first = upper[0]
            for x in range(chans):
                total = [None, None]
                for o in range(2):
                    for g in range(2 * chans):
                        term = coefs[2 * x + o, g, 0] * values[g] + coefs[2 * x + o, g, 1] * swapped[g]
                        total[o] = term if total[o] is None else total[o] + term
                mixed[k, x, n, 0] = jnp.where(first, total[0], pltpu.roll(total[1], rows, 0))
                mixed[k, x, n, 1] = jnp.where(first, pltpu.roll(total[0], rows, 0), total[1])
            return 0

        lax.fori_loop(0, runs, mix_run, 0)

        trade(mixed, ordered, 3, k)

        def send_ordered(b):
            z, core = b // 2, lax.rem(b, 2)
            send(ordered.at[:, lax.rem(z, chans), z // chans], returned, 2, k, b, core)

        (for_all_bands, for_groups)[k](send_ordered)
        returned[k, me] = ordered[k, lax.rem(my_z, chans), my_z // chans, my_core]

    for k in range(2):
        wait_bytes(returned.at[k], bands - 1, recv_sems.at[2, k])
    for t in range(tiles):
        a, b = returned[0, t], returned[1, t]
        keep = left[0]
        pair = (
            jnp.where(keep, a, pltpu.roll(b, HALF, 1)),
            jnp.where(keep, pltpu.roll(a, HALF, 1), b),
        )
        for p in range(2):
            for o in range(2):
                out_ref[2 * p + o, :, t * LANES : (t + 1) * LANES] = pair[p][o * rows : (o + 1) * rows]

    for k in range(2):
        wait_bytes(landed.at[k], bands - 1, send_sems.at[0, k])
        wait_bytes(gathered.at[k], chans - 1, send_sems.at[1, k])
        wait_bytes(returned.at[k], bands - 1, send_sems.at[2, k])
        wait_bytes(ordered.at[k], chans - 1, send_sems.at[3, k])


def on_device(bands, chans, slide_region, row_taps, column_taps, channel_mix):
    channels, rows, cols = slide_region.shape
    tiles = cols // LANES
    height = bands * rows
    vmem = pl.BlockSpec(memory_space=pltpu.VMEM)
    runs = bands // 2 // chans
    traded = pltpu.VMEM((2, chans, 2, runs, 2 * rows, LANES), F32)
    results = pltpu.VMEM((2, chans, runs, 2, 2 * rows, LANES), F32)
    moved = pltpu.VMEM((2, bands, 2 * rows, LANES), F32)
    return pl.pallas_call(
        functools.partial(kernel, bands, chans),
        out_shape=jax.ShapeDtypeStruct(slide_region.shape, F32),
        in_specs=[pl.BlockSpec(memory_space=pl.ANY)] * 4,
        out_specs=vmem,
        scratch_shapes=[
            pltpu.VMEM(slide_region.shape, F32),
            pltpu.VMEM(row_taps.shape, F32),
            pltpu.VMEM(column_taps.shape, F32),
            pltpu.SMEM(channel_mix.shape, F32),
            pltpu.VMEM((8, 2 * height), F32),
            pltpu.VMEM((2, tiles + 2, 2 * rows, LANES), F32),
            pltpu.VMEM((2, 2 * LANES, 3 * LANES), BF16),
            pltpu.VMEM((2, 2 * LANES, 3 * LANES), BF16),
            moved,
            moved,
            pltpu.VMEM((2, 2 * height, height), BF16),
            pltpu.VMEM((2, 2 * height, height), BF16),
            pltpu.VMEM((2 * chans, 2 * chans, 2, 8, LANES), F32),
            traded,
            traded,
            results,
            results,
            moved,
            pltpu.SemaphoreType.DMA((4, 2)),
            pltpu.SemaphoreType.DMA((4, 2)),
            pltpu.SemaphoreType.DMA((4,)),
        ],
        compiler_params=pltpu.CompilerParams(collective_id=0, has_side_effects=True),
    )(slide_region, row_taps, column_taps, channel_mix)


def solution(mesh):
    in_specs = (P("chan", ("groups", "band"), None), P("chan", None), P(), P())
    out_specs = P("chan", ("groups", "band"), None)
    return jax.shard_map(
        functools.partial(on_device, mesh.shape["band"], mesh.shape["chan"]),
        mesh=mesh, in_specs=in_specs, out_specs=out_specs, check_vma=False,
    )
```

time: 150 us -> 142 us (0.947)
  Pallas kernels: 147 us -> 139 us
    pallas_call x1, Pallas kernels: 147 us -> 139 us  [on_device(): pl.pallas_call(functools.partial(kernel, bands, chans), out_shape=jax.Sha...]
where the time goes in v2:
time: 142 us; the launch traced here: 141 us
  Pallas kernels  139 us (98%)
  local copies, waits for them, and re-layouts  1.87 us (1%)
    pallas_call x1, Pallas kernels, on_device(): pl.pallas_call(functools.partial(kernel, bands, chans), out_shape=jax.Sha...  139 us

profile of v2, /device:TPU:40, one launch (start us, length us, event | category | flops | bytes accessed | tf_op | source)
XLA Modules:
  0.0 140.8 jit_solution(14036523523250328397)
XLA Ops:
  0.0 138.9 %shard_map.46 = f32[4,4,8192]{2,1,0:T(4,128)} custom-call(f32[4,4,8192]{2,1,0:T(4,128)} %x_hbm.1, f32[4,257]{1,0:T(4,128)} %row_hbm.1, f32[16,257]{1,0:T(8,128)} %col_hbm.1, f32[16,16]{1,0:T(8,128)} %mix_hbm.1), custom_call_target="tpu_custom_call" | custom-call | tf_op jit(solution)/shard_map/pallas_call | solution.py:273
  139.0 1.9 %copy.6 = f32[4,4,8192]{2,1,0:T(4,128)} copy(f32[4,4,8192]{2,1,0:T(4,128)} %shard_map.46) | data formatting | bytes 1048576

commit v3 on v2

--- a/solution.py
+++ b/solution.py
@@ -38,8 +38,8 @@
 
 
 def kernel(
-    bands, chans, x_hbm, row_hbm, col_hbm, mix_hbm, out_ref,
-    x_ref, row_ref, col_ref, mix_ref, taps, padded, row_high, row_low, sent, landed, col_high, col_low, coefs,
+    bands, chans, x_hbm, row_hbm, col_hbm, mix_hbm, out_hbm,
+    x_ref, row_ref, col_ref, mix_ref, out_ref, taps, padded, row_high, row_low, sent, landed, col_high, col_low, coefs,
     vertical, gathered, mixed, ordered, returned,
     send_sems, recv_sems, own_sems,
 ):
@@ -243,6 +243,7 @@
 
     for k in range(2):
         wait_bytes(returned.at[k], bands - 1, recv_sems.at[2, k])
+    stores = []
     for t in range(tiles):
         a, b = returned[0, t], returned[1, t]
         keep = left[0]
@@ -253,19 +254,28 @@
         for p in range(2):
             for o in range(2):
                 out_ref[2 * p + o, :, t * LANES : (t + 1) * LANES] = pair[p][o * rows : (o + 1) * rows]
+        if (t + 1) % (tiles // 4) == 0:
+            n = t // (tiles // 4)
+            where = pl.ds(n * (tiles // 4) * LANES, (tiles // 4) * LANES)
+            store = pltpu.make_async_copy(
+                out_ref.at[:, :, where], out_hbm.at[:, :, where], own_sems.at[4 + n]
+            )
+            store.start()
+            stores.append(store)
 
     for k in range(2):
         wait_bytes(landed.at[k], bands - 1, send_sems.at[0, k])
         wait_bytes(gathered.at[k], chans - 1, send_sems.at[1, k])
         wait_bytes(returned.at[k], bands - 1, send_sems.at[2, k])
         wait_bytes(ordered.at[k], chans - 1, send_sems.at[3, k])
+    for store in stores:
+        store.wait()
 
 
 def on_device(bands, chans, slide_region, row_taps, column_taps, channel_mix):
     channels, rows, cols = slide_region.shape
     tiles = cols // LANES
     height = bands * rows
-    vmem = pl.BlockSpec(memory_space=pltpu.VMEM)
     runs = bands // 2 // chans
     traded = pltpu.VMEM((2, chans, 2, runs, 2 * rows, LANES), F32)
     results = pltpu.VMEM((2, chans, runs, 2, 2 * rows, LANES), F32)
@@ -274,12 +284,13 @@
         functools.partial(kernel, bands, chans),
         out_shape=jax.ShapeDtypeStruct(slide_region.shape, F32),
         in_specs=[pl.BlockSpec(memory_space=pl.ANY)] * 4,
-        out_specs=vmem,
+        out_specs=pl.BlockSpec(memory_space=pl.ANY),
         scratch_shapes=[
             pltpu.VMEM(slide_region.shape, F32),
             pltpu.VMEM(row_taps.shape, F32),
             pltpu.VMEM(column_taps.shape, F32),
             pltpu.SMEM(channel_mix.shape, F32),
+            pltpu.VMEM(slide_region.shape, F32),
             pltpu.VMEM((8, 2 * height), F32),
             pltpu.VMEM((2, tiles + 2, 2 * rows, LANES), F32),
             pltpu.VMEM((2, 2 * LANES, 3 * LANES), BF16),
@@ -296,7 +307,7 @@
             moved,
             pltpu.SemaphoreType.DMA((4, 2)),
             pltpu.SemaphoreType.DMA((4, 2)),
-            pltpu.SemaphoreType.DMA((4,)),
+            pltpu.SemaphoreType.DMA((8,)),
         ],
         compiler_params=pltpu.CompilerParams(collective_id=0, has_side_effects=True),
     )(slide_region, row_taps, column_taps, channel_mix)

time: 142 us -> 142 us (level)
  no operation moved by 1% of the time
where the time goes in v3:
time: 142 us; the launch traced here: 140 us
  Pallas kernels  138 us (97%)
  local copies, waits for them, and re-layouts  1.87 us (1%)
    pallas_call x1, Pallas kernels, on_device(): pl.pallas_call(functools.partial(kernel, bands, chans), out_shape=jax.Sha...  138 us

profile of v3, /device:TPU:40, one launch (start us, length us, event | category | flops | bytes accessed | tf_op | source)
XLA Modules:
  0.0 140.1 jit_solution(5434954658162338034)
XLA Ops:
  0.0 138.2 %shard_map.46 = f32[4,4,8192]{2,1,0:T(4,128)} custom-call(f32[4,4,8192]{2,1,0:T(4,128)} %x_hbm.1, f32[4,257]{1,0:T(4,128)} %row_hbm.1, f32[16,257]{1,0:T(8,128)} %col_hbm.1, f32[16,16]{1,0:T(8,128)} %mix_hbm.1), custom_call_target="tpu_custom_call" | custom-call | tf_op jit(solution)/shard_map/pallas_call | solution.py:283
  138.2 1.9 %copy.6 = f32[4,4,8192]{2,1,0:T(4,128)} copy(f32[4,4,8192]{2,1,0:T(4,128)} %shard_map.46) | data formatting | bytes 1048576
